TPU v7x, 32 devices: a whole 2x2x4 slice. The times are simulated.
32 devices in a mesh: seq: 8 (over z, y), tp: 4 (over x, core).
Axes of the slice: x: 2, y: 2, z: 4, core: 2. Of those that a mesh axis runs over, the one named last changes fastest.
Arguments:
- query_act: bfloat16 [2048, 4096], P('seq', 'tp'), may hold values from -6 to 6
- key_act: bfloat16 [2048, 1024], P('seq', 'tp'), may hold values from -6 to 6
- value_act: bfloat16 [2048, 1024], P('seq', 'tp'), may hold values from -6 to 6
- attn_out: bfloat16 [2048, 4096], P('seq', 'tp'), may hold values from -6 to 6
- out_grad: bfloat16 [2048, 4096], P('seq', 'tp'), may hold values from -6 to 6
- log_sum: float32 [32, 2048], P('tp', 'seq'), as said below
- positions: int32 [2048], P('seq'), may hold values from 0 to 2047, as said below
- w_query: bfloat16 [4096, 4096], P(None, 'tp'), may hold values from -0.09375 to 0.09375
- w_key: bfloat16 [4096, 1024], P(None, 'tp'), may hold values from -0.09375 to 0.09375
- w_value: bfloat16 [4096, 1024], P(None, 'tp'), may hold values from -0.09375 to 0.09375
Outputs:
- input_grad: bfloat16 [2048, 4096], P('seq', 'tp')
Inputs may be any that keep to these rules, and one draw needn't show every extreme that they name: The rows of one index of seq are two runs of 128 consecutive positions, each run starting at a multiple of 128; all rows together hold every position 0 to 2047 once. log_sum[h, t] lies within 0.5 of log(positions[t] + 1) + 0.5.
All inputs are finite; a program needn't handle non-finite values.
Results may differ from a plain program's by a relative error of at most 0.0057.
Values may be sent and summed in bfloat16 or wider, within the bound.
A program may use at most 64 MiB of HBM per device.

v0:
```python
import functools
import math

import jax
import jax.numpy as jnp
import numpy as np
from jax import lax
from jax.experimental import pallas as pl
from jax.experimental.pallas import tpu as pltpu
from jax.sharding import PartitionSpec as P

HEADS = 32
KV_HEADS = 8
HEAD_DIM = 128
MESH = pl.DeviceIdType.MESH
F32 = jnp.float32
BF16 = jnp.bfloat16


def ring_place(index, n):
    return jnp.where(index % 2 == 0, index // 2, n - 1 - index // 2)


def ring_index(place, n):
    return jnp.where(place < n // 2, 2 * place, 2 * (n - 1 - place) + 1)


def rotate(grad, cosine, sine):
    half = grad.shape[1] // 2
    swapped = jnp.concatenate([grad[:, half:], grad[:, :half]], axis=1)
    return grad * cosine + swapped * sine


def kernel(
    n,
    tp,
    groups,
    repeat,
    q_ref,
    do_ref,
    o_ref,
    kv_ref,
    log_sum_ref,
    qpos_ref,
    cos_ref,
    sin_ref,
    wq_hbm,
    wk_hbm,
    wv_hbm,
    out_ref,
    dq_ref,
    dk_ref,
    dv_ref,
    wq_ref,
    wk_ref,
    wv_ref,
    lse_ref,
    delta_ref,
    terms,
    core_out,
    core_in,
    chip_out,
    chip_in,
    kv_buf,
    acc_out,
    acc_in,
    part,
    own,
    dq_acc,
    gap,
    kv_send,
    kv_recv,
    acc_send,
    acc_recv,
    load_sem,
    core_send,
    core_recv,
    chip_send,
    chip_recv,
):
    rows = q_ref.shape[0]
    half = rows // 2
    dim = q_ref.shape[1] // (groups * repeat)
    scale = dim ** (-0.5)
    log2e = math.log2(math.e)
    place = ring_place(lax.axis_index("seq"), n)
    after = ring_index(lax.rem(place + 1, n), n)
    before = ring_index(lax.rem(place + n - 1, n), n)
    targets = [after if g % 2 == 0 else before for g in range(groups)]

    barrier = pltpu.get_barrier_semaphore()
    for other in (after, before):
        pl.semaphore_signal(barrier, inc=1, device_id={"seq": other}, device_id_type=MESH)
    rank = lax.axis_index("tp")
    chips = tp // 2
    chip, core = rank // 2, lax.rem(rank, 2)
    partner = 2 * chip + 1 - core
    chip_order = [lax.rem(chip + 1 + j, chips) for j in range(chips)]
    peers = [2 * chip_order[j] + core for j in range(chips - 1)]
    for other in [partner] + peers:
        pl.semaphore_signal(barrier, inc=1, device_id={"tp": other}, device_id_type=MESH)
    pl.semaphore_wait(barrier, 2 + chips)

    def kv_copy(g, src, step):
        return pltpu.make_async_remote_copy(
            src_ref=src,
            dst_ref=kv_buf.at[g, step + 1],
            send_sem=kv_send.at[g, step],
            recv_sem=kv_recv.at[g, step + 1],
            device_id={"seq": targets[g]},
            device_id_type=MESH,
        )

    def acc_copy(g, step):
        return pltpu.make_async_remote_copy(
            src_ref=acc_out.at[g, step],
            dst_ref=acc_in.at[g, step + 1],
            send_sem=acc_send.at[g, step],
            recv_sem=acc_recv.at[g, step + 1],
            device_id={"seq": targets[g]},
            device_id_type=MESH,
        )

    def kv_arrival(g, step):
        return pltpu.make_async_remote_copy(
            src_ref=kv_buf.at[g, step],
            dst_ref=kv_buf.at[g, step],
            send_sem=kv_send.at[g, step],
            recv_sem=kv_recv.at[g, step],
            device_id={"seq": targets[g]},
            device_id_type=MESH,
        )

    def acc_arrival(g, step):
        return pltpu.make_async_remote_copy(
            src_ref=acc_in.at[g, step],
            dst_ref=acc_in.at[g, step],
            send_sem=acc_send.at[g, 0],
            recv_sem=acc_recv.at[g, step],
            device_id={"seq": targets[g]},
            device_id_type=MESH,
        )

    for g in range(groups):
        kv_copy(g, kv_ref.at[g], 0).start()

    loads = [
        pltpu.make_async_copy(src, dst, load_sem.at[i])
        for i, (src, dst) in enumerate(((wq_hbm, wq_ref), (wk_hbm, wk_ref), (wv_hbm, wv_ref)))
    ]
    for load in loads:
        load.start()

    lse_ref[...] = log_sum_ref[...] * log2e
    for h in range(groups * repeat):
        cut = slice(h * dim, (h + 1) * dim)
        both = do_ref[:, cut].astype(F32) * o_ref[:, cut].astype(F32)
        delta_ref[h : h + 1, :] = jnp.sum(both.T, axis=0, keepdims=True)
    gap[...] = qpos_ref[...] - lax.broadcasted_iota(jnp.int32, (half, rows), 0).astype(F32)

    def attend(g, block, result, first):
        k = block[0:rows, :]
        v = block[rows : 2 * rows, :]
        tags = block[2 * rows : 2 * rows + 16, :].astype(F32)
        low = jnp.concatenate([tags[0:1, :] * half] * (rows // dim), axis=1)
        high = jnp.concatenate([tags[8:9, :] * half] * (rows // dim), axis=1)
        seen = jnp.concatenate([gap[...] >= low, gap[...] >= high], axis=0)
        kt = k.T
        dk = jnp.zeros((rows, dim), F32)
        dv = jnp.zeros((rows, dim), F32)
        for r in range(repeat):
            h = g * repeat + r
            q = q_ref[:, h * dim : (h + 1) * dim]
            do = do_ref[:, h * dim : (h + 1) * dim]
            nt = (((1,), (1,)), ((), ()))
            s = lax.dot_general(k, q, nt, preferred_element_type=F32)
            p = jnp.exp2(s * (scale * log2e) - lse_ref[h : h + 1, :])
            p = jnp.where(seen, p, 0.0)
            dv += jnp.dot(p.astype(BF16), do, preferred_element_type=F32)
            dp = lax.dot_general(v, do, nt, preferred_element_type=F32)
            ds = (p * (dp - delta_ref[h : h + 1, :])).astype(BF16)
            dk += jnp.dot(ds, q, preferred_element_type=F32)
            dqt = jnp.dot(kt, ds, preferred_element_type=F32)
            if first:
                dq_acc[h] = dqt
            else:
                dq_acc[h] += dqt
        result[g, 0] = dk * scale
        result[g, 1] = dv

    for g in range(groups):
        attend(g, kv_ref.at[g], own, True)

    def turn(step, carry):
        for g in range(groups):
            kv_arrival(g, step).wait_recv()

            @pl.when(step < n - 1)
            def _():
                kv_copy(g, kv_buf.at[g, step], step).start()

        for g in range(groups):
            attend(g, kv_buf.at[g, step], part, False)

            @pl.when(step == 1)
            def _():
                acc_out[g, step] = part[g].astype(BF16)

            @pl.when(step > 1)
            def _():
                acc_arrival(g, step).wait_recv()
                acc_out[g, step] = (part[g] + acc_in[g, step].astype(F32)).astype(BF16)

            acc_copy(g, step).start()
        return carry

    lax.fori_loop(1, n, turn, 0)

    cosine = cos_ref[...]
    sine = sin_ref[...]
    for h in range(groups * repeat):
        dq_ref[:, h * dim : (h + 1) * dim] = rotate(dq_acc[h].T * scale, cosine, sine).astype(BF16)
    cols = out_ref.shape[1]

    def span(block):
        return pl.ds(pl.multiple_of(block * cols, cols), cols)

    for load in loads:
        load.wait()

    def query_terms(block, carry):
        terms[block] = project(dq_ref[...], wq_ref[span(block), :])
        return carry

    lax.fori_loop(0, tp, query_terms, 0)
    for g in range(groups):
        acc_arrival(g, n).wait_recv()
        total = own[g] + acc_in[g, n].astype(F32)
        dk_ref[:, g * dim : (g + 1) * dim] = rotate(total[0], cosine, sine).astype(BF16)
        dv_ref[:, g * dim : (g + 1) * dim] = total[1].astype(BF16)

    def full_terms(block):
        total = terms[block] + project(dk_ref[...], wk_ref[span(block), :])
        return total + project(dv_ref[...], wv_ref[span(block), :])

    def core_copy(j):
        return pltpu.make_async_remote_copy(
            src_ref=core_out.at[j],
            dst_ref=core_in.at[j],
            send_sem=core_send.at[j],
            recv_sem=core_recv.at[j],
            device_id={"tp": partner},
            device_id_type=MESH,
        )

    def chip_copy(j):
        return pltpu.make_async_remote_copy(
            src_ref=chip_out.at[j],
            dst_ref=chip_in.at[j],
            send_sem=chip_send.at[j],
            recv_sem=chip_recv.at[j],
            device_id={"tp": peers[j]},
            device_id_type=MESH,
        )

    for j in range(chips):
        core_out[j] = full_terms(2 * chip_order[j] + 1 - core).astype(BF16)
        core_copy(j).start()
        mine = full_terms(2 * chip_order[j] + core)
        core_copy(j).wait_recv()
        mine = mine + core_in[j].astype(F32)
        if j < chips - 1:
            chip_out[j] = mine.astype(BF16)
            chip_copy(j).start()
        else:
            terms[0] = mine
    total = terms[0]
    for j in range(chips - 1):
        chip_copy(j).wait_recv()
        total = total + chip_in[j].astype(F32)
    out_ref[...] = total.astype(BF16)
    for j in range(chips):
        core_copy(j).wait_send()
    for j in range(chips - 1):
        chip_copy(j).wait_send()

    def drain(step, carry):
        for g in range(groups):
            acc_copy(g, step).wait_send()

            @pl.when(step < n - 1)
            def _():
                kv_copy(g, kv_buf.at[g, step], step).wait_send()

        return carry

    for g in range(groups):
        kv_copy(g, kv_ref.at[g], 0).wait_send()
    lax.fori_loop(1, n, drain, 0)


def project(grads, weight):
    return lax.dot_general(grads, weight, (((1,), (1,)), ((), ())), preferred_element_type=F32)


def shards(
    n, tp, query_act, key_act, value_act, attn_out, out_grad, log_sum, positions, w_query, w_key, w_value
):
    rows, width = query_act.shape
    dim = HEAD_DIM
    repeat = HEADS // KV_HEADS
    groups = key_act.shape[1] // dim
    heads = groups * repeat
    half = rows // 2
    model = w_query.shape[0]
    cols = model // tp
    chips = tp // 2
    place = positions.astype(F32)
    freqs = np.float32(500000.0) ** (-(np.arange(dim // 2, dtype=np.float32) * 2.0 / dim))
    angles = place[:, None] * jnp.asarray(freqs, F32)[None, :]
    cosine = jnp.cos(angles)
    sine = jnp.sin(angles)
    cosine = jnp.concatenate([cosine, cosine], axis=1)
    sine = jnp.concatenate([sine, -sine], axis=1)
    tags = (positions[::half] // half).astype(BF16)
    tags = jnp.broadcast_to(jnp.repeat(tags, 8)[None, :, None], (groups, 16, dim))
    kv = jnp.concatenate(
        [
            key_act.reshape(rows, groups, dim).transpose(1, 0, 2),
            value_act.reshape(rows, groups, dim).transpose(1, 0, 2),
            tags,
        ],
        axis=1,
    )
    vmem = pl.BlockSpec(memory_space=pltpu.VMEM)
    hbm = pl.BlockSpec(memory_space=pl.ANY)
    return pl.pallas_call(
        functools.partial(kernel, n, tp, groups, repeat),
        out_shape=jax.ShapeDtypeStruct((rows, cols), BF16),
        in_specs=[vmem] * 8 + [hbm] * 3,
        out_specs=vmem,
        scratch_shapes=[
            pltpu.VMEM((rows, width), BF16),
            pltpu.VMEM((rows, groups * dim), BF16),
            pltpu.VMEM((rows, groups * dim), BF16),
            pltpu.VMEM(w_query.shape, BF16),
            pltpu.VMEM(w_key.shape, BF16),
            pltpu.VMEM(w_value.shape, BF16),
            pltpu.VMEM((heads, rows), F32),
            pltpu.VMEM((heads, rows), F32),
            pltpu.VMEM((tp, rows, cols), F32),
            pltpu.VMEM((chips, rows, cols), BF16),
            pltpu.VMEM((chips, rows, cols), BF16),
            pltpu.VMEM((chips - 1, rows, cols), BF16),
            pltpu.VMEM((chips - 1, rows, cols), BF16),
            pltpu.VMEM((groups, n, 2 * rows + 16, dim), BF16),
            pltpu.VMEM((groups, n, 2, rows, dim), BF16),
            pltpu.VMEM((groups, n + 1, 2, rows, dim), BF16),
            pltpu.VMEM((groups, 2, rows, dim), F32),
            pltpu.VMEM((groups, 2, rows, dim), F32),
            pltpu.VMEM((heads, dim, rows), F32),
            pltpu.VMEM((half, rows), F32),
            pltpu.SemaphoreType.DMA((groups, n + 1)),
            pltpu.SemaphoreType.DMA((groups, n + 1)),
            pltpu.SemaphoreType.DMA((groups, n + 1)),
            pltpu.SemaphoreType.DMA((groups, n + 1)),
            pltpu.SemaphoreType.DMA((3,)),
            pltpu.SemaphoreType.DMA((chips,)),
            pltpu.SemaphoreType.DMA((chips,)),
            pltpu.SemaphoreType.DMA((chips - 1,)),
            pltpu.SemaphoreType.DMA((chips - 1,)),
        ],
        compiler_params=pltpu.CompilerParams(
            collective_id=0, has_side_effects=True, vmem_limit_bytes=58 * 1024 * 1024
        ),
    )(
        query_act,
        out_grad,
        attn_out,
        kv,
        log_sum,
        place[None, :],
        cosine,
        sine,
        w_query,
        w_key,
        w_value,
    )


def solution(mesh):
    return jax.shard_map(
        functools.partial(shards, mesh.shape["seq"], mesh.shape["tp"]),
        mesh=mesh,
        in_specs=(
            P("seq", "tp"),
            P("seq", "tp"),
            P("seq", "tp"),
            P("seq", "tp"),
            P("seq", "tp"),
            P("tp", "seq"),
            P("seq"),
            P(None, "tp"),
            P(None, "tp"),
            P(None, "tp"),
        ),
        out_specs=P("seq", "tp"),
        check_vma=False,
    )
```

profile of v0, /device:TPU:0, one launch (start us, length us, event | category | flops | bytes accessed | tf_op | source)
XLA Modules:
  0.0 75.7 jit_solution(369282407876676744)
XLA Ops:
  0.0 0.8 %slice.3 = s32[2]{0:T(128)S(1)} slice(s32[256]{0:T(256)} %param.17), slice={[0:256:128]} | slice | bytes 16 | tf_op jit(solution)/shard_map/slice | solution.py:325
  0.8 0.1 broadcast_in_dim.15
  0.9 0.1 reshape.11
  0.9 0.7 convert_element_type.7
  1.6 0.0 copy-start
  1.6 1.0 %copy.12 = bf16[256,256]{0,1:T(8,128)(2,1)S(1)} copy(bf16[256,256]{1,0:T(8,128)(2,1)} %param.12) | data formatting | bytes 262144 | tf_op args[1]
  2.6 0.1 copy.13
  2.8 1.0 %copy.14 = bf16[256,256]{0,1:T(8,128)(2,1)S(1)} copy(bf16[256,256]{1,0:T(8,128)(2,1)} %param.13) | data formatting | bytes 262144 | tf_op args[2]
  3.8 0.1 copy.15
  3.9 0.8 %maximum_maximum_fusion.kv_ref = bf16[2,528,128]{2,1,0:T(8,128)(2,1)} fusion(bf16[2,256,128]{2,1,0:T(8,128)(2,1)S(1)} %bitcast.8, bf16[2,256,128]{2,1,0:T(8,128)(2,1)S(1)} %bitcast.7, bf16[528]{0:T(1024)(128)(2,1)S(1)} %pad.6.clone), kind=kLoop, calls=%fused_computation | loop fusion | flops 811008 | bytes 533536 | tf_op jit(solution)/shard_map/concatenate | solution.py:327
  4.8 1.2 %multiply_sine_fusion = (f32[256,64]{1,0:T(8,128)S(1)}, f32[256,64]{1,0:T(8,128)S(1)}, f32[256,64]{1,0:T(8,128)S(1)}) fusion(f32[64]{0:T(128)} %constant.18.clone, f32[256]{0:T(256)S(1)} %convert_element_type.7), kind=kLoop, calls=%fused_computation.1 | loop fusion | flops 32768 | bytes 197888 | tf_op jit(solution)/shard_map/sin | solution.py:322
  5.9 0.8 %pad_maximum_fusion = (f32[256,128]{1,0:T(8,128)}, f32[256,128]{1,0:T(8,128)}) fusion(f32[256,64]{1,0:T(8,128)S(1)} %get-tuple-element.7, f32[256,64]{1,0:T(8,128)S(1)} %get-tuple-element.6, f32[256,64]{1,0:T(8,128)S(1)} %get-tuple-element.5), kind=kLoop, calls=%fused_computation.3 | loop fusion | flops 65536 | bytes 458752 | tf_op jit(solution)/shard_map/concatenate | solution.py:323
  6.8 0.0 copy-done
  6.8 67.1 %shard_map.109 = bf16[256,1024]{1,0:T(8,128)(2,1)} custom-call(bf16[256,1024]{1,0:T(8,128)(2,1)} %q_ref.1, bf16[256,1024]{1,0:T(8,128)(2,1)} %do_ref.1, bf16[256,1024]{1,0:T(8,128)(2,1)} %o_ref.1, bf16[2,528,128]{2,1,0:T(8,128)(2,1)} %maximum_maximum_fusion.kv_ref, f32[8,256]{1,0:T(8,128)} %log_sum_ref.1, f32[1,256]{1,0:T(1,128)} %bitcast.9, ...), custom_call_target="tpu_custom_call" | custom-call | tf_op jit(solution)/shard_map/pallas_call | solution.py:337
  73.9 1.9 %copy.17 = bf16[256,1024]{1,0:T(8,128)(2,1)} copy(bf16[256,1024]{1,0:T(8,128)(2,1)} %shard_map.109) | data formatting | bytes 1048576
  (2 shorter events, 0.0 us)
Async XLA Ops:
  1.6 5.2 %copy-start = (f32[256]{0:T(256)}, f32[256]{0:T(256)S(1)}, u32[]{:S(2)}) copy-start(f32[256]{0:T(256)S(1)} %convert_element_type.7) | copy-start | bytes 3076
where the time goes:
time: 76.1 us; the launch traced here: 75.7 us
  Pallas kernels  67.1 us (88%)
  local copies, waits for them, and re-layouts  5.05 us (7%)
  other arithmetic  3.56 us (5%)
    pallas_call x1, Pallas kernels, shards(): pl.pallas_call(functools.partial(kernel, n, tp, groups, repeat), out_shap...  67.1 us
    unnamed x5, local copies, waits for them, and re-layouts  3.88 us

commit v1 on v0

v1 whole, which is shorter than its diff:
```python
import functools
import math

import jax
import jax.numpy as jnp
import numpy as np
from jax import lax
from jax.experimental import pallas as pl
from jax.experimental.pallas import tpu as pltpu
from jax.sharding import PartitionSpec as P

HEADS = 32
KV_HEADS = 8
HEAD_DIM = 128
MESH = pl.DeviceIdType.MESH
F32 = jnp.float32
BF16 = jnp.bfloat16
PIECE = 256
VMEM_LIMIT = 58 * 1024 * 1024


def ring_place(index, n):
    return jnp.where(index % 2 == 0, index // 2, n - 1 - index // 2)


def ring_index(place, n):
    return jnp.where(place < n // 2, 2 * place, 2 * (n - 1 - place) + 1)


def rotate(grad, cosine, sine):
    half = grad.shape[0] // 2
    first, second = grad[:half], grad[half:]
    return jnp.concatenate([first * cosine + second * sine, second * cosine - first * sine], axis=0)


def kernel(
    n,
    tp,
    groups,
    repeat,
    q_hbm,
    do_hbm,
    o_hbm,
    k_hbm,
    v_hbm,
    log_sum_ref,
    qpos_ref,
    freq_ref,
    wq_hbm,
    wk_hbm,
    wv_hbm,
    out_hbm,
    q_ref,
    do_ref,
    o_ref,
    dq_ref,
    dk_ref,
    dv_ref,
    wq_ref,
    wk_ref,
    wv_ref,
    lse_ref,
    delta_ref,
    pos_ref,
    terms,
    core_out,
    core_in,
    chip_out,
    chip_in,
    kv_buf,
    acc_out,
    acc_in,
    part,
    own,
    dq_acc,
    out_ref,
    kv_send,
    kv_recv,
    acc_send,
    acc_recv,
    load_sem,
    in_sem,
    kvin_sem,
    out_sem,
    core_send,
    core_recv,
    chip_send,
    chip_recv,
):
    rows, width = q_ref.shape
    half = rows // 2
    dim = width // (groups * repeat)
    scale = dim ** (-0.5)
    log2e = math.log2(math.e)
    place = ring_place(lax.axis_index("seq"), n)
    after = ring_index(lax.rem(place + 1, n), n)
    before = ring_index(lax.rem(place + n - 1, n), n)
    targets = [after if g % 2 == 0 else before for g in range(groups)]

    barrier = pltpu.get_barrier_semaphore()
    for other in (after, before):
        pl.semaphore_signal(barrier, inc=1, device_id={"seq": other}, device_id_type=MESH)
    rank = lax.axis_index("tp")
    chips = tp // 2
    chip, core = rank // 2, lax.rem(rank, 2)
    partner = 2 * chip + 1 - core
    chip_order = [lax.rem(chip + 1 + j, chips) for j in range(chips)]
    peers = [2 * chip_order[j] + core for j in range(chips - 1)]
    for other in [partner] + peers:
        pl.semaphore_signal(barrier, inc=1, device_id={"tp": other}, device_id_type=MESH)

    kv_loads = []
    for g in range(groups):
        cut = pl.ds(g * dim, dim)
        for i, src in enumerate((k_hbm, v_hbm)):
            kv_loads.append(
                pltpu.make_async_copy(
                    src.at[:, cut], kv_buf.at[g, 0, pl.ds(i * rows, rows), :], kvin_sem.at[g, i]
                )
            )
            kv_loads[-1].start()
    in_loads = [
        pltpu.make_async_copy(src, dst, in_sem.at[i])
        for i, (src, dst) in enumerate(((q_hbm, q_ref), (do_hbm, do_ref), (o_hbm, o_ref)))
    ]
    for load in in_loads:
        load.start()
    loads = [
        pltpu.make_async_copy(src, dst, load_sem.at[i])
        for i, (src, dst) in enumerate(((wq_hbm, wq_ref), (wk_hbm, wk_ref), (wv_hbm, wv_ref)))
    ]
    for load in loads:
        load.start()

    qpos = qpos_ref[...].astype(F32)
    pos_ref[...] = qpos
    first_tag = jnp.broadcast_to(qpos[:, 0:1] * (1.0 / half), (8, dim))
    second_tag = jnp.broadcast_to(qpos[:, half : half + 1] * (1.0 / half), (8, dim))
    tags = jnp.concatenate([first_tag, second_tag], axis=0).astype(BF16)
    for g in range(groups):
        kv_buf[g, 0, 2 * rows : 2 * rows + 16, :] = tags

    def kv_copy(g, step):
        return pltpu.make_async_remote_copy(
            src_ref=kv_buf.at[g, step],
            dst_ref=kv_buf.at[g, step + 1],
            send_sem=kv_send.at[g, step],
            recv_sem=kv_recv.at[g, step + 1],
            device_id={"seq": targets[g]},
            device_id_type=MESH,
        )

    def acc_copy(g, step):
        return pltpu.make_async_remote_copy(
            src_ref=acc_out.at[g, step],
            dst_ref=acc_in.at[g, step + 1],
            send_sem=acc_send.at[g, step],
            recv_sem=acc_recv.at[g, step + 1],
            device_id={"seq": targets[g]},
            device_id_type=MESH,
        )

    def kv_arrival(g, step):
        return pltpu.make_async_remote_copy(
            src_ref=kv_buf.at[g, step],
            dst_ref=kv_buf.at[g, step],
            send_sem=kv_send.at[g, step],
            recv_sem=kv_recv.at[g, step],
            device_id={"seq": targets[g]},
            device_id_type=MESH,
        )

    def acc_arrival(g, step):
        return pltpu.make_async_remote_copy(
            src_ref=acc_in.at[g, step],
            dst_ref=acc_in.at[g, step],
            send_sem=acc_send.at[g, 0],
            recv_sem=acc_recv.at[g, step],
            device_id={"seq": targets[g]},
            device_id_type=MESH,
        )

    for load in kv_loads:
        load.wait()
    pl.semaphore_wait(barrier, 2 + chips)
    for g in range(groups):
        kv_copy(g, 0).start()

    lse_ref[...] = log_sum_ref[...] * log2e
    for load in in_loads:
        load.wait()
    for h in range(groups * repeat):
        cut = slice(h * dim, (h + 1) * dim)
        both = do_ref[:, cut].astype(F32) * o_ref[:, cut].astype(F32)
        delta_ref[h : h + 1, :] = jnp.sum(both.T, axis=0, keepdims=True)

    def attend(g, block, result, first):
        k = block[0:rows, :]
        v = block[rows : 2 * rows, :]
        tags = block[2 * rows : 2 * rows + 16, :].astype(F32)
        low = jnp.concatenate([tags[0:1, :] * half] * (rows // dim), axis=1)
        high = jnp.concatenate([tags[8:9, :] * half] * (rows // dim), axis=1)
        if first:
            gap = pos_ref[...] - lax.broadcasted_iota(jnp.int32, (half, rows), 0).astype(F32)
            seen = jnp.concatenate([gap >= low, gap >= high], axis=0)
        else:
            low = jnp.where(pos_ref[...] >= low, 0.0, 1e30)
            high = jnp.where(pos_ref[...] >= high, 0.0, 1e30)
        kt = k.T
        dk = jnp.zeros((rows, dim), F32)
        dv = jnp.zeros((rows, dim), F32)
        for r in range(repeat):
            h = g * repeat + r
            q = q_ref[:, h * dim : (h + 1) * dim]
            do = do_ref[:, h * dim : (h + 1) * dim]
            nt = (((1,), (1,)), ((), ()))
            s = lax.dot_general(k, q, nt, preferred_element_type=F32) * (scale * log2e)
            lse = lse_ref[h : h + 1, :]
            if first:
                p = jnp.where(seen, jnp.exp2(s - lse), 0.0)
            else:
                p = jnp.concatenate(
                    [jnp.exp2(s[:half] - (lse + low)), jnp.exp2(s[half:] - (lse + high))], axis=0
                )
            dv += jnp.dot(p.astype(BF16), do, preferred_element_type=F32)
            dp = lax.dot_general(v, do, nt, preferred_element_type=F32)
            ds = (p * (dp - delta_ref[h : h + 1, :])).astype(BF16)
            dk += jnp.dot(ds, q, preferred_element_type=F32)
            dqt = jnp.dot(kt, ds, preferred_element_type=F32)
            if first:
                dq_acc[h] = dqt
            else:
                dq_acc[h] += dqt
        result[g, 0] = dk * scale
        result[g, 1] = dv

    for g in range(groups):
        attend(g, kv_buf.at[g, 0], own, True)

    def turn(step, carry):
        for g in range(groups):
            kv_arrival(g, step).wait_recv()

            @pl.when(step < n - 1)
            def _():
                kv_copy(g, step).start()

        for g in range(groups):
            attend(g, kv_buf.at[g, step], part, False)

            @pl.when(step == 1)
            def _():
                acc_out[g, step] = part[g].astype(BF16)

            @pl.when(step > 1)
            def _():
                acc_arrival(g, step).wait_recv()
                acc_out[g, step] = (part[g] + acc_in[g, step].astype(F32)).astype(BF16)

            acc_copy(g, step).start()
        return carry

    lax.fori_loop(1, n, turn, 0)

    angles = freq_ref[...] * pos_ref[...]
    cosine = jnp.cos(angles)
    sine = jnp.sin(angles)
    for h in range(groups * repeat):
        dq_ref[:, h * dim : (h + 1) * dim] = rotate(dq_acc[h] * scale, cosine, sine).T.astype(BF16)
    cols = out_hbm.shape[1]
    pieces = max(1, cols // PIECE)
    wide = cols // pieces

    def span(block, piece):
        return pl.ds(pl.multiple_of(block * cols + piece * wide, wide), wide)

    for load in loads:
        load.wait()
    far = [2 * chip_order[j] + 1 - core for j in range(chips)]
    near = [2 * chip_order[j] + core for j in range(chips)]

    def query_terms(piece, carry):
        for j in range(chips):
            for i, block in enumerate((far[j], near[j])):
                terms[2 * j + i, piece] = project(dq_ref[...], wq_ref[span(block, piece), :])
        return carry

    lax.fori_loop(0, pieces, query_terms, 0)
    for g in range(groups):
        acc_arrival(g, n).wait_recv()
        total = own[g] + acc_in[g, n].astype(F32)
        dk_ref[:, g * dim : (g + 1) * dim] = rotate(total[0].T, cosine, sine).T.astype(BF16)
        dv_ref[:, g * dim : (g + 1) * dim] = total[1].astype(BF16)

    def full_terms(slot, block, piece):
        total = terms[slot, piece] + project(dk_ref[...], wk_ref[span(block, piece), :])
        return total + project(dv_ref[...], wv_ref[span(block, piece), :])

    def core_copy(j, piece):
        return pltpu.make_async_remote_copy(
            src_ref=core_out.at[j, piece],
            dst_ref=core_in.at[j, piece],
            send_sem=core_send.at[j, piece],
            recv_sem=core_recv.at[j, piece],
            device_id={"tp": partner},
            device_id_type=MESH,
        )

    def chip_copy(j, piece):
        return pltpu.make_async_remote_copy(
            src_ref=chip_out.at[j, piece],
            dst_ref=chip_in.at[j, piece],
            send_sem=chip_send.at[j, piece],
            recv_sem=chip_recv.at[j, piece],
            device_id={"tp": peers[j]},
            device_id_type=MESH,
        )

    def relay(j, piece):
        core_copy(j, piece).wait_recv()
        mine = terms[2 * j + 1, piece] + core_in[j, piece].astype(F32)
        if j < chips - 1:
            chip_out[j, piece] = mine.astype(BF16)
            chip_copy(j, piece).start()
        else:
            terms[2 * j + 1, piece] = mine

    for j in range(chips):
        for piece in range(pieces):
            core_out[j, piece] = full_terms(2 * j, far[j], piece).astype(BF16)
            core_copy(j, piece).start()
            terms[2 * j + 1, piece] = full_terms(2 * j + 1, near[j], piece)
            if piece > 0:
                relay(j, piece - 1)
        relay(j, pieces - 1)

    def out_copy(piece):
        cut = pl.ds(piece * wide, wide)
        return pltpu.make_async_copy(out_ref.at[:, cut], out_hbm.at[:, cut], out_sem.at[piece])

    for piece in range(pieces):
        total = terms[2 * chips - 1, piece]
        for j in range(chips - 1):
            chip_copy(j, piece).wait_recv()
            total = total + chip_in[j, piece].astype(F32)
        out_ref[:, piece * wide : (piece + 1) * wide] = total.astype(BF16)
        out_copy(piece).start()
    for piece in range(pieces):
        for j in range(chips):
            core_copy(j, piece).wait_send()
        for j in range(chips - 1):
            chip_copy(j, piece).wait_send()

    def drain(step, carry):
        for g in range(groups):
            kv_copy(g, step).wait_send()

            @pl.when(step > 0)
            def _():
                acc_copy(g, step).wait_send()

        return carry

    lax.fori_loop(0, n - 1, drain, 0)
    for g in range(groups):
        acc_copy(g, n - 1).wait_send()
    for piece in range(pieces):
        out_copy(piece).wait()


def project(grads, weight):
    return lax.dot_general(grads, weight, (((1,), (1,)), ((), ())), preferred_element_type=F32)


def shards(
    n, tp, query_act, key_act, value_act, attn_out, out_grad, log_sum, positions, w_query, w_key, w_value
):
    rows, width = query_act.shape
    dim = HEAD_DIM
    repeat = HEADS // KV_HEADS
    groups = key_act.shape[1] // dim
    heads = groups * repeat
    half = rows // 2
    model = w_query.shape[0]
    cols = model // tp
    chips = tp // 2
    freqs = np.float32(500000.0) ** (-(np.arange(dim // 2, dtype=np.float32) * 2.0 / dim))
    pieces = max(1, cols // PIECE)
    wide = cols // pieces
    vmem = pl.BlockSpec(memory_space=pltpu.VMEM)
    hbm = pl.BlockSpec(memory_space=pl.ANY)
    return pl.pallas_call(
        functools.partial(kernel, n, tp, groups, repeat),
        out_shape=jax.ShapeDtypeStruct((rows, cols), BF16),
        in_specs=[hbm] * 5 + [vmem] * 3 + [hbm] * 3,
        out_specs=hbm,
        scratch_shapes=[
            pltpu.VMEM((rows, width), BF16),
            pltpu.VMEM((rows, width), BF16),
            pltpu.VMEM((rows, width), BF16),
            pltpu.VMEM((rows, width), BF16),
            pltpu.VMEM((rows, groups * dim), BF16),
            pltpu.VMEM((rows, groups * dim), BF16),
            pltpu.VMEM(w_query.shape, BF16),
            pltpu.VMEM(w_key.shape, BF16),
            pltpu.VMEM(w_value.shape, BF16),
            pltpu.VMEM((heads, rows), F32),
            pltpu.VMEM((heads, rows), F32),
            pltpu.VMEM((1, rows), F32),
            pltpu.VMEM((tp, pieces, rows, wide), F32),
            pltpu.VMEM((chips, pieces, rows, wide), BF16),
            pltpu.VMEM((chips, pieces, rows, wide), BF16),
            pltpu.VMEM((chips - 1, pieces, rows, wide), BF16),
            pltpu.VMEM((chips - 1, pieces, rows, wide), BF16),
            pltpu.VMEM((groups, n, 2 * rows + 16, dim), BF16),
            pltpu.VMEM((groups, n, 2, rows, dim), BF16),
            pltpu.VMEM((groups, n + 1, 2, rows, dim), BF16),
            pltpu.VMEM((groups, 2, rows, dim), F32),
            pltpu.VMEM((groups, 2, rows, dim), F32),
            pltpu.VMEM((heads, dim, rows), F32),
            pltpu.VMEM((rows, cols), BF16),
            pltpu.SemaphoreType.DMA((groups, n + 1)),
            pltpu.SemaphoreType.DMA((groups, n + 1)),
            pltpu.SemaphoreType.DMA((groups, n + 1)),
            pltpu.SemaphoreType.DMA((groups, n + 1)),
            pltpu.SemaphoreType.DMA((3,)),
            pltpu.SemaphoreType.DMA((3,)),
            pltpu.SemaphoreType.DMA((groups, 2)),
            pltpu.SemaphoreType.DMA((pieces,)),
            pltpu.SemaphoreType.DMA((chips, pieces)),
            pltpu.SemaphoreType.DMA((chips, pieces)),
            pltpu.SemaphoreType.DMA((chips - 1, pieces)),
            pltpu.SemaphoreType.DMA((chips - 1, pieces)),
        ],
        compiler_params=pltpu.CompilerParams(
            collective_id=0, has_side_effects=True, vmem_limit_bytes=VMEM_LIMIT
        ),
    )(
        query_act,
        out_grad,
        attn_out,
        key_act,
        value_act,
        log_sum,
        positions[None, :],
        jnp.asarray(freqs)[:, None],
        w_query,
        w_key,
        w_value,
    )


def solution(mesh):
    return jax.shard_map(
        functools.partial(shards, mesh.shape["seq"], mesh.shape["tp"]),
        mesh=mesh,
        in_specs=(
            P("seq", "tp"),
            P("seq", "tp"),
            P("seq", "tp"),
            P("seq", "tp"),
            P("seq", "tp"),
            P("tp", "seq"),
            P("seq"),
            P(None, "tp"),
            P(None, "tp"),
            P(None, "tp"),
        ),
        out_specs=P("seq", "tp"),
        check_vma=False,
    )
```

time: 76.1 us -> 71.6 us (0.941)
  other arithmetic: 3.56 us -> 0 us
  local copies, waits for them, and re-layouts: 5.05 us -> 1.87 us
  Pallas kernels: 67.1 us -> 69.5 us
    pallas_call x1, Pallas kernels: 67.1 us -> 69.5 us  [shards(): pl.pallas_call(functools.partial(kernel, n, tp, groups, repeat), out_shap...]
    unnamed x5 -> x1, local copies, waits for them, and re-layouts: 3.88 us -> 1.87 us
    concatenate x2 -> x0, other arithmetic: 1.68 us -> none  [the longest x1 0.85 us: shards(): jnp.concatenate([key_act.reshape(rows, groups, dim).transpose(1, 0, 2), v...]
    sin x1 -> x0, other arithmetic: 1.19 us -> none  [shards(): sine = jnp.sin(angles)]
    slice x1 -> x0, local copies, waits for them, and re-layouts: 0.76 us -> none  [shards(): tags = (positions[::half] // half).astype(BF16)]
where the time goes in v1:
time: 71.6 us; the launch traced here: 71.3 us
  Pallas kernels  69.5 us (97%)
  local copies, waits for them, and re-layouts  1.87 us (3%)
    pallas_call x1, Pallas kernels, shards(): pl.pallas_call(functools.partial(kernel, n, tp, groups, repeat), out_shap...  69.5 us
    unnamed x1, local copies, waits for them, and re-layouts  1.87 us

profile of v1, /device:TPU:0, one launch (start us, length us, event | category | flops | bytes accessed | tf_op | source)
XLA Modules:
  0.0 71.3 jit_solution(6361224831826242165)
XLA Ops:
  0.0 69.5 %shard_map.109 = bf16[256,1024]{1,0:T(8,128)(2,1)} custom-call(bf16[256,1024]{1,0:T(8,128)(2,1)} %q_hbm.1, bf16[256,1024]{1,0:T(8,128)(2,1)} %do_hbm.1, bf16[256,1024]{1,0:T(8,128)(2,1)} %o_hbm.1, bf16[256,256]{1,0:T(8,128)(2,1)} %k_hbm.1, bf16[256,256]{1,0:T(8,128)(2,1)} %v_hbm.1, f32[8,256]{1,0:T(8,128)} %log_sum_ref.1, s32[1,256]{1,0:T(1,128)} %bitcast.1, ...), custom_call_target="tpu_custom_call" | custom-call | tf_op jit(solution)/shard_map/pallas_call | solution.py:392
  69.5 1.9 %copy.13 = bf16[256,1024]{1,0:T(8,128)(2,1)} copy(bf16[256,1024]{1,0:T(8,128)(2,1)} %shard_map.109) | data formatting | bytes 1048576

commit v2 on v1

--- a/solution.py
+++ b/solution.py
@@ -17,6 +17,19 @@
 BF16 = jnp.bfloat16
 PIECE = 256
 VMEM_LIMIT = 58 * 1024 * 1024
+OUT = pltpu.VMEM
+ORDER = (
+    ("take", 0, 0),
+    ("take", 1, 1),
+    ("take", 0, 1),
+    ("work", 0, 0),
+    ("give", 0, 1),
+    ("take", 1, 0),
+    ("work", 1, 0),
+    ("give", 1, 0),
+    ("give", 0, 0),
+    ("give", 1, 1),
+)
 
 
 def ring_place(index, n):
@@ -49,7 +62,7 @@
     wq_hbm,
     wk_hbm,
     wv_hbm,
-    out_hbm,
+    out_ref,
     q_ref,
     do_ref,
     o_ref,
@@ -73,7 +86,6 @@
     part,
     own,
     dq_acc,
-    out_ref,
     kv_send,
     kv_recv,
     acc_send,
@@ -81,7 +93,6 @@
     load_sem,
     in_sem,
     kvin_sem,
-    out_sem,
     core_send,
     core_recv,
     chip_send,
@@ -129,8 +140,6 @@
         pltpu.make_async_copy(src, dst, load_sem.at[i])
         for i, (src, dst) in enumerate(((wq_hbm, wq_ref), (wk_hbm, wk_ref), (wv_hbm, wv_ref)))
     ]
-    for load in loads:
-        load.start()
 
     qpos = qpos_ref[...].astype(F32)
     pos_ref[...] = qpos
@@ -140,42 +149,45 @@
     for g in range(groups):
         kv_buf[g, 0, 2 * rows : 2 * rows + 16, :] = tags
 
-    def kv_copy(g, step):
-        return pltpu.make_async_remote_copy(
-            src_ref=kv_buf.at[g, step],
-            dst_ref=kv_buf.at[g, step + 1],
-            send_sem=kv_send.at[g, step],
-            recv_sem=kv_recv.at[g, step + 1],
+    def slot(g, step, i):
+        return kv_buf.at[g, step, pl.ds(i * rows, rows + 16 * i), :]
+
+    def kv_copy(g, step, i):
+        return pltpu.make_async_remote_copy(
+            src_ref=slot(g, step, i),
+            dst_ref=slot(g, step + 1, i),
+            send_sem=kv_send.at[g, i, step],
+            recv_sem=kv_recv.at[g, i, step + 1],
             device_id={"seq": targets[g]},
             device_id_type=MESH,
         )
 
-    def acc_copy(g, step):
-        return pltpu.make_async_remote_copy(
-            src_ref=acc_out.at[g, step],
-            dst_ref=acc_in.at[g, step + 1],
-            send_sem=acc_send.at[g, step],
-            recv_sem=acc_recv.at[g, step + 1],
+    def acc_copy(g, step, i):
+        return pltpu.make_async_remote_copy(
+            src_ref=acc_out.at[g, step, i],
+            dst_ref=acc_in.at[g, step + 1, i],
+            send_sem=acc_send.at[g, i, step],
+            recv_sem=acc_recv.at[g, i, step + 1],
             device_id={"seq": targets[g]},
             device_id_type=MESH,
         )
 
-    def kv_arrival(g, step):
-        return pltpu.make_async_remote_copy(
-            src_ref=kv_buf.at[g, step],
-            dst_ref=kv_buf.at[g, step],
-            send_sem=kv_send.at[g, step],
-            recv_sem=kv_recv.at[g, step],
+    def kv_arrival(g, step, i):
+        return pltpu.make_async_remote_copy(
+            src_ref=slot(g, step, i),
+            dst_ref=slot(g, step, i),
+            send_sem=kv_send.at[g, i, step],
+            recv_sem=kv_recv.at[g, i, step],
             device_id={"seq": targets[g]},
             device_id_type=MESH,
         )
 
-    def acc_arrival(g, step):
-        return pltpu.make_async_remote_copy(
-            src_ref=acc_in.at[g, step],
-            dst_ref=acc_in.at[g, step],
-            send_sem=acc_send.at[g, 0],
-            recv_sem=acc_recv.at[g, step],
+    def acc_arrival(g, step, i):
+        return pltpu.make_async_remote_copy(
+            src_ref=acc_in.at[g, step, i],
+            dst_ref=acc_in.at[g, step, i],
+            send_sem=acc_send.at[g, i, 0],
+            recv_sem=acc_recv.at[g, i, step],
             device_id={"seq": targets[g]},
             device_id_type=MESH,
         )
@@ -183,8 +195,11 @@
     for load in kv_loads:
         load.wait()
     pl.semaphore_wait(barrier, 2 + chips)
-    for g in range(groups):
-        kv_copy(g, 0).start()
+    for i in range(2):
+        for g in range(groups):
+            kv_copy(g, 0, i).start()
+    for load in loads:
+        load.start()
 
     lse_ref[...] = log_sum_ref[...] * log2e
     for load in in_loads:
@@ -237,27 +252,35 @@
     for g in range(groups):
         attend(g, kv_buf.at[g, 0], own, True)
 
+    def take(g, i, step):
+        kv_arrival(g, step, i).wait_recv()
+
+        @pl.when(step < n - 1)
+        def _():
+            kv_copy(g, step, i).start()
+
+    def give(g, i, step):
+        @pl.when(step == 1)
+        def _():
+            acc_out[g, step, i] = part[g, i].astype(BF16)
+
+        @pl.when(step > 1)
+        def _():
+            acc_arrival(g, step, i).wait_recv()
+            acc_out[g, step, i] = (part[g, i] + acc_in[g, step, i].astype(F32)).astype(BF16)
+
+        acc_copy(g, step, i).start()
+
     def turn(step, carry):
-        for g in range(groups):
-            kv_arrival(g, step).wait_recv()
-
-            @pl.when(step < n - 1)
-            def _():
-                kv_copy(g, step).start()
-
-        for g in range(groups):
-            attend(g, kv_buf.at[g, step], part, False)
-
-            @pl.when(step == 1)
-            def _():
-                acc_out[g, step] = part[g].astype(BF16)
-
-            @pl.when(step > 1)
-            def _():
-                acc_arrival(g, step).wait_recv()
-                acc_out[g, step] = (part[g] + acc_in[g, step].astype(F32)).astype(BF16)
-
-            acc_copy(g, step).start()
+        for act, g, i in ORDER:
+            if g >= groups:
+                continue
+            if act == "take":
+                take(g, i, step)
+            elif act == "work":
+                attend(g, kv_buf.at[g, step], part, False)
+            else:
+                give(g, i, step)
         return carry
 
     lax.fori_loop(1, n, turn, 0)
@@ -267,7 +290,7 @@
     sine = jnp.sin(angles)
     for h in range(groups * repeat):
         dq_ref[:, h * dim : (h + 1) * dim] = rotate(dq_acc[h] * scale, cosine, sine).T.astype(BF16)
-    cols = out_hbm.shape[1]
+    cols = out_ref.shape[1]
     pieces = max(1, cols // PIECE)
     wide = cols // pieces
 
@@ -287,7 +310,8 @@
 
     lax.fori_loop(0, pieces, query_terms, 0)
     for g in range(groups):
-        acc_arrival(g, n).wait_recv()
+        for i in range(2):
+            acc_arrival(g, n, i).wait_recv()
         total = own[g] + acc_in[g, n].astype(F32)
         dk_ref[:, g * dim : (g + 1) * dim] = rotate(total[0].T, cosine, sine).T.astype(BF16)
         dv_ref[:, g * dim : (g + 1) * dim] = total[1].astype(BF16)
@@ -329,14 +353,9 @@
         for piece in range(pieces):
             core_out[j, piece] = full_terms(2 * j, far[j], piece).astype(BF16)
             core_copy(j, piece).start()
+        for piece in range(pieces):
             terms[2 * j + 1, piece] = full_terms(2 * j + 1, near[j], piece)
-            if piece > 0:
-                relay(j, piece - 1)
-        relay(j, pieces - 1)
-
-    def out_copy(piece):
-        cut = pl.ds(piece * wide, wide)
-        return pltpu.make_async_copy(out_ref.at[:, cut], out_hbm.at[:, cut], out_sem.at[piece])
+            relay(j, piece)
 
     for piece in range(pieces):
         total = terms[2 * chips - 1, piece]
@@ -344,7 +363,6 @@
             chip_copy(j, piece).wait_recv()
             total = total + chip_in[j, piece].astype(F32)
         out_ref[:, piece * wide : (piece + 1) * wide] = total.astype(BF16)
-        out_copy(piece).start()
     for piece in range(pieces):
         for j in range(chips):
             core_copy(j, piece).wait_send()
@@ -353,19 +371,19 @@
 
     def drain(step, carry):
         for g in range(groups):
-            kv_copy(g, step).wait_send()
-
-            @pl.when(step > 0)
-            def _():
-                acc_copy(g, step).wait_send()
+            for i in range(2):
+                kv_copy(g, step, i).wait_send()
+
+                @pl.when(step > 0)
+                def _():
+                    acc_copy(g, step, i).wait_send()
 
         return carry
 
     lax.fori_loop(0, n - 1, drain, 0)
     for g in range(groups):
-        acc_copy(g, n - 1).wait_send()
-    for piece in range(pieces):
-        out_copy(piece).wait()
+        for i in range(2):
+            acc_copy(g, n - 1, i).wait_send()
 
 
 def project(grads, weight):
@@ -391,9 +409,9 @@
     hbm = pl.BlockSpec(memory_space=pl.ANY)
     return pl.pallas_call(
         functools.partial(kernel, n, tp, groups, repeat),
-        out_shape=jax.ShapeDtypeStruct((rows, cols), BF16),
+        out_shape=OUT((rows, cols), BF16),
         in_specs=[hbm] * 5 + [vmem] * 3 + [hbm] * 3,
-        out_specs=hbm,
+        out_specs=vmem,
         scratch_shapes=[
             pltpu.VMEM((rows, width), BF16),
             pltpu.VMEM((rows, width), BF16),
@@ -418,15 +436,13 @@
             pltpu.VMEM((groups, 2, rows, dim), F32),
             pltpu.VMEM((groups, 2, rows, dim), F32),
             pltpu.VMEM((heads, dim, rows), F32),
-            pltpu.VMEM((rows, cols), BF16),
-            pltpu.SemaphoreType.DMA((groups, n + 1)),
-            pltpu.SemaphoreType.DMA((groups, n + 1)),
-            pltpu.SemaphoreType.DMA((groups, n + 1)),
-            pltpu.SemaphoreType.DMA((groups, n + 1)),
+            pltpu.SemaphoreType.DMA((groups, 2, n + 1)),
+            pltpu.SemaphoreType.DMA((groups, 2, n + 1)),
+            pltpu.SemaphoreType.DMA((groups, 2, n + 1)),
+            pltpu.SemaphoreType.DMA((groups, 2, n + 1)),
             pltpu.SemaphoreType.DMA((3,)),
             pltpu.SemaphoreType.DMA((3,)),
             pltpu.SemaphoreType.DMA((groups, 2)),
-            pltpu.SemaphoreType.DMA((pieces,)),
             pltpu.SemaphoreType.DMA((chips, pieces)),
             pltpu.SemaphoreType.DMA((chips, pieces)),
             pltpu.SemaphoreType.DMA((chips - 1, pieces)),

time: 71.6 us -> 66.8 us (0.933)
  Pallas kernels: 69.5 us -> 65.8 us
  local copies, waits for them, and re-layouts: 1.87 us -> 0.8 us
    pallas_call x1, Pallas kernels: 69.5 us -> 65.8 us  [shards(): pl.pallas_call(functools.partial(kernel, n, tp, groups, repeat), out_shap...]
    unnamed x1, local copies, waits for them, and re-layouts: 1.87 us -> 0.8 us
where the time goes in v2:
time: 66.8 us; the launch traced here: 66.6 us
  Pallas kernels  65.8 us (99%)
  local copies, waits for them, and re-layouts  0.8 us (1%)
    pallas_call x1, Pallas kernels, shards(): pl.pallas_call(functools.partial(kernel, n, tp, groups, repeat), out_shap...  65.8 us

profile of v2, /device:TPU:0, one launch (start us, length us, event | category | flops | bytes accessed | tf_op | source)
XLA Modules:
  0.0 66.6 jit_solution(17912734047289578338)
XLA Ops:
  0.0 65.8 %shard_map.109 = bf16[256,1024]{1,0:T(8,128)(2,1)S(1)} custom-call(bf16[256,1024]{1,0:T(8,128)(2,1)} %q_hbm.1, bf16[256,1024]{1,0:T(8,128)(2,1)} %do_hbm.1, bf16[256,1024]{1,0:T(8,128)(2,1)} %o_hbm.1, bf16[256,256]{1,0:T(8,128)(2,1)} %k_hbm.1, bf16[256,256]{1,0:T(8,128)(2,1)} %v_hbm.1, f32[8,256]{1,0:T(8,128)} %log_sum_ref.1, s32[1,256]{1,0:T(1,128)} %bitcast.1, ...), custom_call_target="tpu_custom_call" | custom-call | tf_op jit(solution)/shard_map/pallas_call | solution.py:410
  65.8 0.8 %copy.13 = bf16[256,1024]{1,0:T(8,128)(2,1)} copy(bf16[256,1024]{1,0:T(8,128)(2,1)S(1)} %shard_map.109) | data formatting | bytes 1048576

commit v3 on v2

v3 whole, which is shorter than its diff:
```python
import functools
import math

import jax
import jax.numpy as jnp
import numpy as np
from jax import lax
from jax.experimental import pallas as pl
from jax.experimental.pallas import tpu as pltpu
from jax.sharding import PartitionSpec as P

HEADS = 32
KV_HEADS = 8
HEAD_DIM = 128
MESH = pl.DeviceIdType.MESH
F32 = jnp.float32
BF16 = jnp.bfloat16
PIECE = 512
VMEM_LIMIT = 58 * 1024 * 1024
OUT = pltpu.VMEM


def ring_place(index, n):
    return jnp.where(index % 2 == 0, index // 2, n - 1 - index // 2)


def ring_index(place, n):
    return jnp.where(place < n // 2, 2 * place, 2 * (n - 1 - place) + 1)


def rotate(grad, cosine, sine):
    half = grad.shape[0] // 2
    first, second = grad[:half], grad[half:]
    return jnp.concatenate([first * cosine + second * sine, second * cosine - first * sine], axis=0)


def kernel(
    n,
    tp,
    groups,
    repeat,
    q_hbm,
    do_hbm,
    o_hbm,
    k_hbm,
    v_hbm,
    log_sum_hbm,
    qpos_hbm,
    freq_hbm,
    wq_hbm,
    wk_hbm,
    wv_hbm,
    out_ref,
    q_ref,
    do_ref,
    o_ref,
    dq_ref,
    dk_ref,
    dv_ref,
    wq_ref,
    wk_ref,
    wv_ref,
    log_sum_ref,
    qpos_ref,
    freq_ref,
    lse_ref,
    delta_ref,
    pos_ref,
    cos_ref,
    sin_ref,
    terms,
    core_out,
    core_in,
    chip_out,
    chip_in,
    kv_buf,
    acc_out,
    acc_in,
    part,
    own,
    dq_acc,
    kv_send,
    kv_recv,
    acc_send,
    acc_recv,
    load_sem,
    in_sem,
    kvin_sem,
    small_sem,
    core_send,
    core_recv,
    chip_send,
    chip_recv,
):
    rows, width = q_ref.shape
    half = rows // 2
    dim = width // (groups * repeat)
    scale = dim ** (-0.5)
    log2e = math.log2(math.e)
    place = ring_place(lax.axis_index("seq"), n)
    after = ring_index(lax.rem(place + 1, n), n)
    before = ring_index(lax.rem(place + n - 1, n), n)
    targets = [after if g % 2 == 0 else before for g in range(groups)]

    barrier = pltpu.get_barrier_semaphore()
    for other in (after, before):
        pl.semaphore_signal(barrier, inc=1, device_id={"seq": other}, device_id_type=MESH)
    rank = lax.axis_index("tp")
    chips = tp // 2
    chip, core = rank // 2, lax.rem(rank, 2)
    partner = 2 * chip + 1 - core
    chip_order = [lax.rem(chip + 1 + j, chips) for j in range(chips)]
    peers = [2 * chip_order[j] + core for j in range(chips - 1)]
    for other in [partner] + peers:
        pl.semaphore_signal(barrier, inc=1, device_id={"tp": other}, device_id_type=MESH)

    small = [
        pltpu.make_async_copy(src, dst, small_sem.at[i])
        for i, (src, dst) in enumerate(
            ((qpos_hbm, qpos_ref), (log_sum_hbm, log_sum_ref), (freq_hbm, freq_ref))
        )
    ]
    small[0].start()
    kv_loads = []
    for g in range(groups):
        cut = pl.ds(g * dim, dim)
        for i, src in enumerate((k_hbm, v_hbm)):
            for r in range(2):
                load = pltpu.make_async_copy(
                    src.at[pl.ds(r * half, half), cut],
                    kv_buf.at[g, 0, r, pl.ds(i * half, half), :],
                    kvin_sem.at[g, i, r],
                )
                load.start()
                kv_loads.append(load)
    small[1].start()
    small[2].start()
    in_loads = [
        pltpu.make_async_copy(src, dst, in_sem.at[i])
        for i, (src, dst) in enumerate(((q_hbm, q_ref), (do_hbm, do_ref), (o_hbm, o_ref)))
    ]
    for load in in_loads:
        load.start()
    loads = [
        pltpu.make_async_copy(src, dst, load_sem.at[i])
        for i, (src, dst) in enumerate(((wq_hbm, wq_ref), (wk_hbm, wk_ref), (wv_hbm, wv_ref)))
    ]

    small[0].wait()
    qpos = qpos_ref[...].astype(F32)
    pos_ref[...] = qpos
    for r in range(2):
        tag = jnp.broadcast_to(qpos[:, r * half : r * half + 1] * (1.0 / half), (8, dim)).astype(BF16)
        for g in range(groups):
            kv_buf[g, 0, r, 2 * half : 2 * half + 8, :] = tag

    def kv_copy(g, step, i):
        return pltpu.make_async_remote_copy(
            src_ref=kv_buf.at[g, step, i],
            dst_ref=kv_buf.at[g, step + 1, i],
            send_sem=kv_send.at[g, i, step],
            recv_sem=kv_recv.at[g, i, step + 1],
            device_id={"seq": targets[g]},
            device_id_type=MESH,
        )

    def acc_copy(g, step, i):
        return pltpu.make_async_remote_copy(
            src_ref=acc_out.at[g, step, i],
            dst_ref=acc_in.at[g, step + 1, i],
            send_sem=acc_send.at[g, i, step],
            recv_sem=acc_recv.at[g, i, step + 1],
            device_id={"seq": targets[g]},
            device_id_type=MESH,
        )

    def kv_arrival(g, step, i):
        return pltpu.make_async_remote_copy(
            src_ref=kv_buf.at[g, step, i],
            dst_ref=kv_buf.at[g, step, i],
            send_sem=kv_send.at[g, i, step],
            recv_sem=kv_recv.at[g, i, step],
            device_id={"seq": targets[g]},
            device_id_type=MESH,
        )

    def acc_arrival(g, step, i):
        return pltpu.make_async_remote_copy(
            src_ref=acc_in.at[g, step, i],
            dst_ref=acc_in.at[g, step, i],
            send_sem=acc_send.at[g, i, 0],
            recv_sem=acc_recv.at[g, i, step],
            device_id={"seq": targets[g]},
            device_id_type=MESH,
        )

    for load in kv_loads:
        load.wait()
    pl.semaphore_wait(barrier, 2 + chips)
    for i in range(2):
        for g in range(groups):
            kv_copy(g, 0, i).start()
    for load in loads:
        load.start()

    small[1].wait()
    small[2].wait()
    lse_ref[...] = log_sum_ref[...] * log2e
    for load in in_loads:
        load.wait()
    for h in range(groups * repeat):
        cut = slice(h * dim, (h + 1) * dim)
        both = do_ref[:, cut].astype(F32) * o_ref[:, cut].astype(F32)
        delta_ref[h : h + 1, :] = jnp.sum(both.T, axis=0, keepdims=True)

    angles = freq_ref[:, 0:1] * pos_ref[...]
    cos_ref[...] = jnp.cos(angles)
    sin_ref[...] = jnp.sin(angles)

    def run(r):
        return slice(r * half, (r + 1) * half)

    def attend(g, r, block, result, first):
        k = block[0:half, :]
        v = block[half : 2 * half, :]
        tag = block[2 * half : 2 * half + 8, :].astype(F32)
        low = jnp.concatenate([tag[0:1, :] * half] * (rows // dim), axis=1)
        if first:
            gap = pos_ref[...] - lax.broadcasted_iota(jnp.int32, (half, rows), 0).astype(F32)
            seen = gap >= low
        else:
            hide = jnp.where(pos_ref[...] >= low, 0.0, 1e30)
        kt = k.T
        dk = jnp.zeros((half, dim), F32)
        dv = jnp.zeros((half, dim), F32)
        for c in range(repeat):
            h = g * repeat + c
            q = q_ref[:, h * dim : (h + 1) * dim]
            do = do_ref[:, h * dim : (h + 1) * dim]
            nt = (((1,), (1,)), ((), ()))
            s = lax.dot_general(k, q, nt, preferred_element_type=F32) * (scale * log2e)
            lse = lse_ref[h : h + 1, :]
            if first:
                p = jnp.where(seen, jnp.exp2(s - lse), 0.0)
            else:
                p = jnp.exp2(s - (lse + hide))
            dv += jnp.dot(p.astype(BF16), do, preferred_element_type=F32)
            dp = lax.dot_general(v, do, nt, preferred_element_type=F32)
            ds = (p * (dp - delta_ref[h : h + 1, :])).astype(BF16)
            dk += jnp.dot(ds, q, preferred_element_type=F32)
            dqt = jnp.dot(kt, ds, preferred_element_type=F32)
            if first and r == 0:
                dq_acc[h] = dqt
            else:
                dq_acc[h] += dqt
        result[g, 0, run(r), :] = dk * scale
        result[g, 1, run(r), :] = dv

    for r in range(2):
        for g in range(groups):
            attend(g, r, kv_buf.at[g, 0, r], own, True)

    def take(g, i, step):
        kv_arrival(g, step, i).wait_recv()

        @pl.when(step < n - 1)
        def _():
            kv_copy(g, step, i).start()

    def give(g, i, step):
        @pl.when(step == 1)
        def _():
            acc_out[g, step, i] = part[g, :, run(i), :].astype(BF16)

        @pl.when(step > 1)
        def _():
            acc_arrival(g, step, i).wait_recv()
            total = part[g, :, run(i), :] + acc_in[g, step, i].astype(F32)
            acc_out[g, step, i] = total.astype(BF16)

        acc_copy(g, step, i).start()

    def turn(step, carry):
        for r in range(2):
            for g in range(groups):
                take(g, r, step)
            for g in range(groups):
                attend(g, r, kv_buf.at[g, step, r], part, False)
            for g in range(groups):
                give(g, r, step)
        return carry

    lax.fori_loop(1, n, turn, 0)

    cosine = cos_ref[...]
    sine = sin_ref[...]
    for h in range(groups * repeat):
        dq_ref[:, h * dim : (h + 1) * dim] = rotate(dq_acc[h] * scale, cosine, sine).T.astype(BF16)
    cols = out_ref.shape[1]
    pieces = max(1, cols // PIECE)
    wide = cols // pieces

    def span(block, piece):
        return pl.ds(pl.multiple_of(block * cols + piece * wide, wide), wide)

    for load in loads:
        load.wait()
    far = [2 * chip_order[j] + 1 - core for j in range(chips)]
    near = [2 * chip_order[j] + core for j in range(chips)]

    def query_terms(slot, block, piece):
        both = project(dq_ref[...], wq_ref[span(block, piece), :])
        for r in range(2):
            terms[slot, r, piece] = both[run(r)]

    def finish_grads(r):
        for g in range(groups):
            acc_arrival(g, n, r).wait_recv()
            total = own[g, :, run(r), :] + acc_in[g, n, r].astype(F32)
            cut = slice(g * dim, (g + 1) * dim)
            turned = rotate(total[0].T, cosine[:, run(r)], sine[:, run(r)]).T
            dk_ref[run(r), cut] = turned.astype(BF16)
            dv_ref[run(r), cut] = total[1].astype(BF16)

    def full_terms(slot, block, r, piece):
        total = terms[slot, r, piece] + project(dk_ref[run(r), :], wk_ref[span(block, piece), :])
        return total + project(dv_ref[run(r), :], wv_ref[span(block, piece), :])

    def core_copy(j, r, piece):
        return pltpu.make_async_remote_copy(
            src_ref=core_out.at[j, r, piece],
            dst_ref=core_in.at[j, r, piece],
            send_sem=core_send.at[j, r, piece],
            recv_sem=core_recv.at[j, r, piece],
            device_id={"tp": partner},
            device_id_type=MESH,
        )

    def chip_copy(j, r, piece):
        return pltpu.make_async_remote_copy(
            src_ref=chip_out.at[j, r, piece],
            dst_ref=chip_in.at[j, r, piece],
            send_sem=chip_send.at[j, r, piece],
            recv_sem=chip_recv.at[j, r, piece],
            device_id={"tp": peers[j]},
            device_id_type=MESH,
        )

    def relay(j, r, piece):
        core_copy(j, r, piece).wait_recv()
        mine = terms[2 * j + 1, r, piece] + core_in[j, r, piece].astype(F32)
        if j < chips - 1:
            chip_out[j, r, piece] = mine.astype(BF16)
            chip_copy(j, r, piece).start()
        else:
            terms[2 * j + 1, r, piece] = mine

    def share(j, r):
        for piece in range(pieces):
            if r == 0:
                query_terms(2 * j, far[j], piece)
            core_out[j, r, piece] = full_terms(2 * j, far[j], r, piece).astype(BF16)
            core_copy(j, r, piece).start()
        for piece in range(pieces):
            if r == 0:
                query_terms(2 * j + 1, near[j], piece)
            terms[2 * j + 1, r, piece] = full_terms(2 * j + 1, near[j], r, piece)
            relay(j, r, piece)

    for r in range(2):
        finish_grads(r)
        for j in range(chips - 1):
            share(j, r)
    for r in range(2):
        share(chips - 1, r)

    for r in range(2):
        for piece in range(pieces):
            total = terms[2 * chips - 1, r, piece]
            for j in range(chips - 1):
                chip_copy(j, r, piece).wait_recv()
                total = total + chip_in[j, r, piece].astype(F32)
            out_ref[run(r), piece * wide : (piece + 1) * wide] = total.astype(BF16)
    for r in range(2):
        for piece in range(pieces):
            for j in range(chips):
                core_copy(j, r, piece).wait_send()
            for j in range(chips - 1):
                chip_copy(j, r, piece).wait_send()

    def drain(step, carry):
        for g in range(groups):
            for i in range(2):
                kv_copy(g, step, i).wait_send()

                @pl.when(step > 0)
                def _():
                    acc_copy(g, step, i).wait_send()

        return carry

    lax.fori_loop(0, n - 1, drain, 0)
    for g in range(groups):
        for i in range(2):
            acc_copy(g, n - 1, i).wait_send()


def project(grads, weight):
    return lax.dot_general(grads, weight, (((1,), (1,)), ((), ())), preferred_element_type=F32)


def shards(
    n, tp, query_act, key_act, value_act, attn_out, out_grad, log_sum, positions, w_query, w_key, w_value
):
    rows, width = query_act.shape
    dim = HEAD_DIM
    repeat = HEADS // KV_HEADS
    groups = key_act.shape[1] // dim
    heads = groups * repeat
    half = rows // 2
    model = w_query.shape[0]
    cols = model // tp
    chips = tp // 2
    freqs = np.float32(500000.0) ** (-(np.arange(dim // 2, dtype=np.float32) * 2.0 / dim))
    pieces = max(1, cols // PIECE)
    wide = cols // pieces
    vmem = pl.BlockSpec(memory_space=pltpu.VMEM)
    hbm = pl.BlockSpec(memory_space=pl.ANY)
    return pl.pallas_call(
        functools.partial(kernel, n, tp, groups, repeat),
        out_shape=OUT((rows, cols), BF16),
        in_specs=[hbm] * 11,
        out_specs=vmem,
        scratch_shapes=[
            pltpu.VMEM((rows, width), BF16),
            pltpu.VMEM((rows, width), BF16),
            pltpu.VMEM((rows, width), BF16),
            pltpu.VMEM((rows, width), BF16),
            pltpu.VMEM((rows, groups * dim), BF16),
            pltpu.VMEM((rows, groups * dim), BF16),
            pltpu.VMEM(w_query.shape, BF16),
            pltpu.VMEM(w_key.shape, BF16),
            pltpu.VMEM(w_value.shape, BF16),
            pltpu.VMEM((heads, rows), F32),
            pltpu.VMEM((1, rows), jnp.int32),
            pltpu.VMEM((dim // 2, dim), F32),
            pltpu.VMEM((heads, rows), F32),
            pltpu.VMEM((heads, rows), F32),
            pltpu.VMEM((1, rows), F32),
            pltpu.VMEM((dim // 2, rows), F32),
            pltpu.VMEM((dim // 2, rows), F32),
            pltpu.VMEM((tp, 2, pieces, half, wide), F32),
            pltpu.VMEM((chips, 2, pieces, half, wide), BF16),
            pltpu.VMEM((chips, 2, pieces, half, wide), BF16),
            pltpu.VMEM((chips - 1, 2, pieces, half, wide), BF16),
            pltpu.VMEM((chips - 1, 2, pieces, half, wide), BF16),
            pltpu.VMEM((groups, n, 2, 2 * half + 8, dim), BF16),
            pltpu.VMEM((groups, n, 2, 2, half, dim), BF16),
            pltpu.VMEM((groups, n + 1, 2, 2, half, dim), BF16),
            pltpu.VMEM((groups, 2, rows, dim), F32),
            pltpu.VMEM((groups, 2, rows, dim), F32),
            pltpu.VMEM((heads, dim, rows), F32),
            pltpu.SemaphoreType.DMA((groups, 2, n + 1)),
            pltpu.SemaphoreType.DMA((groups, 2, n + 1)),
            pltpu.SemaphoreType.DMA((groups, 2, n + 1)),
            pltpu.SemaphoreType.DMA((groups, 2, n + 1)),
            pltpu.SemaphoreType.DMA((3,)),
            pltpu.SemaphoreType.DMA((3,)),
            pltpu.SemaphoreType.DMA((groups, 2, 2)),
            pltpu.SemaphoreType.DMA((3,)),
            pltpu.SemaphoreType.DMA((chips, 2, pieces)),
            pltpu.SemaphoreType.DMA((chips, 2, pieces)),
            pltpu.SemaphoreType.DMA((chips - 1, 2, pieces)),
            pltpu.SemaphoreType.DMA((chips - 1, 2, pieces)),
        ],
        compiler_params=pltpu.CompilerParams(
            collective_id=0, has_side_effects=True, vmem_limit_bytes=VMEM_LIMIT
        ),
    )(
        query_act,
        out_grad,
        attn_out,
        key_act,
        value_act,
        log_sum,
        positions[None, :],
        jnp.broadcast_to(jnp.asarray(freqs)[:, None], (dim // 2, dim)),
        w_query,
        w_key,
        w_value,
    )


def solution(mesh):
    return jax.shard_map(
        functools.partial(shards, mesh.shape["seq"], mesh.shape["tp"]),
        mesh=mesh,
        in_specs=(
            P("seq", "tp"),
            P("seq", "tp"),
            P("seq", "tp"),
            P("seq", "tp"),
            P("seq", "tp"),
            P("tp", "seq"),
            P("seq"),
            P(None, "tp"),
            P(None, "tp"),
            P(None, "tp"),
        ),
        out_specs=P("seq", "tp"),
        check_vma=False,
    )
```

time: 66.8 us -> 66.3 us (level)
  Pallas kernels: 65.8 us -> 64 us
  local copies, waits for them, and re-layouts: 0.8 us -> 2.14 us
    pallas_call x1, Pallas kernels: 65.8 us -> 64 us  [shards(): pl.pallas_call(functools.partial(kernel, n, tp, groups, repeat), out_shap...]
    broadcast_in_dim x0 -> x1, local copies, waits for them, and re-layouts: none -> 1.34 us  [shards(): jnp.broadcast_to(jnp.asarray(freqs)[:, None], (dim // 2, dim))]
where the time goes in v3:
time: 66.3 us; the launch traced here: 66.1 us
  Pallas kernels  64 us (97%)
  local copies, waits for them, and re-layouts  2.14 us (3%)
    pallas_call x1, Pallas kernels, shards(): pl.pallas_call(functools.partial(kernel, n, tp, groups, repeat), out_shap...  64 us
    broadcast_in_dim x1, local copies, waits for them, and re-layouts, shards(): jnp.broadcast_to(jnp.asarray(freqs)[:, None], (dim // 2, dim))  1.34 us

profile of v3, /device:TPU:0, one launch (start us, length us, event | category | flops | bytes accessed | tf_op | source)
XLA Modules:
  0.0 66.1 jit_solution(1180919510162310029)
XLA Ops:
  0.0 1.3 %broadcast_in_dim.10.freq_hbm = f32[64,128]{1,0:T(8,128)} broadcast(f32[64]{0:T(128)} %constant.2.clone), dimensions={0} | broadcast | bytes 33024 | tf_op jit(solution)/shard_map/broadcast_in_dim | solution.py:487
  1.3 64.0 %shard_map.109 = bf16[256,1024]{1,0:T(8,128)(2,1)S(1)} custom-call(bf16[256,1024]{1,0:T(8,128)(2,1)} %q_hbm.1, bf16[256,1024]{1,0:T(8,128)(2,1)} %do_hbm.1, bf16[256,1024]{1,0:T(8,128)(2,1)} %o_hbm.1, bf16[256,256]{1,0:T(8,128)(2,1)} %k_hbm.1, bf16[256,256]{1,0:T(8,128)(2,1)} %v_hbm.1, f32[8,256]{1,0:T(8,128)} %log_sum_hbm.1, s32[1,256]{1,0:T(1,128)} %bitcast.1, ...), custom_call_target="tpu_custom_call" | custom-call | tf_op jit(solution)/shard_map/pallas_call | solution.py:429
  65.3 0.8 %copy.13 = bf16[256,1024]{1,0:T(8,128)(2,1)} copy(bf16[256,1024]{1,0:T(8,128)(2,1)S(1)} %shard_map.109) | data formatting | bytes 1048576

commit v4 on v3

--- a/solution.py
+++ b/solution.py
@@ -44,9 +44,9 @@
     o_hbm,
     k_hbm,
     v_hbm,
-    log_sum_hbm,
-    qpos_hbm,
-    freq_hbm,
+    log_sum_ref,
+    qpos_ref,
+    freq_ref,
     wq_hbm,
     wk_hbm,
     wv_hbm,
@@ -60,9 +60,6 @@
     wq_ref,
     wk_ref,
     wv_ref,
-    log_sum_ref,
-    qpos_ref,
-    freq_ref,
     lse_ref,
     delta_ref,
     pos_ref,
@@ -86,7 +83,6 @@
     load_sem,
     in_sem,
     kvin_sem,
-    small_sem,
     core_send,
     core_recv,
     chip_send,
@@ -114,13 +110,6 @@
     for other in [partner] + peers:
         pl.semaphore_signal(barrier, inc=1, device_id={"tp": other}, device_id_type=MESH)
 
-    small = [
-        pltpu.make_async_copy(src, dst, small_sem.at[i])
-        for i, (src, dst) in enumerate(
-            ((qpos_hbm, qpos_ref), (log_sum_hbm, log_sum_ref), (freq_hbm, freq_ref))
-        )
-    ]
-    small[0].start()
     kv_loads = []
     for g in range(groups):
         cut = pl.ds(g * dim, dim)
@@ -133,8 +122,6 @@
                 )
                 load.start()
                 kv_loads.append(load)
-    small[1].start()
-    small[2].start()
     in_loads = [
         pltpu.make_async_copy(src, dst, in_sem.at[i])
         for i, (src, dst) in enumerate(((q_hbm, q_ref), (do_hbm, do_ref), (o_hbm, o_ref)))
@@ -146,7 +133,6 @@
         for i, (src, dst) in enumerate(((wq_hbm, wq_ref), (wk_hbm, wk_ref), (wv_hbm, wv_ref)))
     ]
 
-    small[0].wait()
     qpos = qpos_ref[...].astype(F32)
     pos_ref[...] = qpos
     for r in range(2):
@@ -203,8 +189,6 @@
     for load in loads:
         load.start()
 
-    small[1].wait()
-    small[2].wait()
     lse_ref[...] = log_sum_ref[...] * log2e
     for load in in_loads:
         load.wait()
@@ -429,7 +413,7 @@
     return pl.pallas_call(
         functools.partial(kernel, n, tp, groups, repeat),
         out_shape=OUT((rows, cols), BF16),
-        in_specs=[hbm] * 11,
+        in_specs=[hbm] * 5 + [vmem] * 3 + [hbm] * 3,
         out_specs=vmem,
         scratch_shapes=[
             pltpu.VMEM((rows, width), BF16),
@@ -441,9 +425,6 @@
             pltpu.VMEM(w_query.shape, BF16),
             pltpu.VMEM(w_key.shape, BF16),
             pltpu.VMEM(w_value.shape, BF16),
-            pltpu.VMEM((heads, rows), F32),
-            pltpu.VMEM((1, rows), jnp.int32),
-            pltpu.VMEM((dim // 2, dim), F32),
             pltpu.VMEM((heads, rows), F32),
             pltpu.VMEM((heads, rows), F32),
             pltpu.VMEM((1, rows), F32),
@@ -467,7 +448,6 @@
             pltpu.SemaphoreType.DMA((3,)),
             pltpu.SemaphoreType.DMA((3,)),
             pltpu.SemaphoreType.DMA((groups, 2, 2)),
-            pltpu.SemaphoreType.DMA((3,)),
             pltpu.SemaphoreType.DMA((chips, 2, pieces)),
             pltpu.SemaphoreType.DMA((chips, 2, pieces)),
             pltpu.SemaphoreType.DMA((chips - 1, 2, pieces)),

time: 66.3 us -> 67.1 us (1.012)
  Pallas kernels: 64 us -> 64.8 us
    pallas_call x1, Pallas kernels: 64 us -> 64.8 us  [shards(): pl.pallas_call(functools.partial(kernel, n, tp, groups, repeat), out_shap...]
where the time goes in v4:
time: 67.1 us; the launch traced here: 66.9 us
  Pallas kernels  64.8 us (97%)
  local copies, waits for them, and re-layouts  2.14 us (3%)
    pallas_call x1, Pallas kernels, shards(): pl.pallas_call(functools.partial(kernel, n, tp, groups, repeat), out_shap...  64.8 us
    broadcast_in_dim x1, local copies, waits for them, and re-layouts, shards(): jnp.broadcast_to(jnp.asarray(freqs)[:, None], (dim // 2, dim))  1.34 us

profile of v4, /device:TPU:0, one launch (start us, length us, event | category | flops | bytes accessed | tf_op | source)
XLA Modules:
  0.0 66.9 jit_solution(5801665841234573601)
XLA Ops:
  0.0 1.3 %broadcast_in_dim.10.freq_ref = f32[64,128]{1,0:T(8,128)} broadcast(f32[64]{0:T(128)} %constant.2.clone), dimensions={0} | broadcast | bytes 33024 | tf_op jit(solution)/shard_map/broadcast_in_dim | solution.py:467
  1.3 64.8 %shard_map.109 = bf16[256,1024]{1,0:T(8,128)(2,1)S(1)} custom-call(bf16[256,1024]{1,0:T(8,128)(2,1)} %q_hbm.1, bf16[256,1024]{1,0:T(8,128)(2,1)} %do_hbm.1, bf16[256,1024]{1,0:T(8,128)(2,1)} %o_hbm.1, bf16[256,256]{1,0:T(8,128)(2,1)} %k_hbm.1, bf16[256,256]{1,0:T(8,128)(2,1)} %v_hbm.1, f32[8,256]{1,0:T(8,128)} %log_sum_ref.1, s32[1,256]{1,0:T(1,128)} %bitcast.1, ...), custom_call_target="tpu_custom_call" | custom-call | tf_op jit(solution)/shard_map/pallas_call | solution.py:413
  66.1 0.8 %copy.13 = bf16[256,1024]{1,0:T(8,128)(2,1)} copy(bf16[256,1024]{1,0:T(8,128)(2,1)S(1)} %shard_map.109) | data formatting | bytes 1048576
